TPU v7x, 256 devices: a whole 4x4x8 slice. The times are simulated.
256 devices in a mesh: zero: 16 (over y, x), width: 16 (over z, core).
Axes of the slice: x: 4, y: 4, z: 8, core: 2. Of those that a mesh axis runs over, the one named last changes fastest.
Arguments:
- train_gate: float32 [5120, 13824], P('zero', 'width'), may hold values from -0.125 to 0.125
- drift_gate: float32 [5120, 13824], P('zero', 'width'), may hold values from -0.078125 to 0.078125
- spread_gate: float32 [5120, 13824], P('zero', 'width'), may hold values from -0.078125 to 0.078125
- train_up: float32 [5120, 13824], P('zero', 'width'), may hold values from -0.125 to 0.125
- drift_up: float32 [5120, 13824], P('zero', 'width'), may hold values from -0.078125 to 0.078125
- spread_up: float32 [5120, 13824], P('zero', 'width'), may hold values from -0.078125 to 0.078125
- norm_gain: float32 [5120], P('zero'), may hold values from 0.25 to 1.75
Outputs:
- serving_gate: bfloat16 [5120, 13824], P(None, 'width')
- serving_up: bfloat16 [5120, 13824], P(None, 'width')
- factor_gate: float32 [13824], P('width')
- factor_up: float32 [13824], P('width')
All inputs are finite; a program needn't handle non-finite values. Where the computation divides by a largest or mean magnitude, that divisor is 1e-20 or more.
Results may differ from a plain program's by a relative error of at most 0.001.
Values may be sent and summed in bfloat16 or wider, within the bound.
A program may use at most 192 MiB of HBM per device.

v0:
```python
import jax
import jax.numpy as jnp
from jax import lax
from jax.sharding import PartitionSpec as P

learn_rate = 0.3
hold_rate = 0.9


def sent_to_all(array, axis):
    count = lax.axis_size(axis)
    return lax.all_to_all(
        jnp.broadcast_to(array[None], (count, *array.shape)), axis, 0, 0, tiled=True
    )


def taken_together(array, axis):
    return sent_to_all(array, axis).max(axis=0)


def together(arrays, axis):
    ends = [0]
    for a in arrays:
        ends.append(ends[-1] + a.size)
    so_far = taken_together(jnp.concatenate([a.ravel() for a in arrays]), axis)
    return tuple((so_far[b:e].reshape(a.shape) for a, b, e in zip(arrays, ends, ends[1:])))


def sent_together(arrays, axis, dim, along):
    both = jnp.concatenate(arrays, axis=along)
    filled, at, outs = (lax.all_gather(both, axis, axis=dim, tiled=True), 0, [])
    for a in arrays:
        outs.append(lax.slice_in_dim(filled, at, at + a.shape[along], axis=along))
        at += a.shape[along]
    return tuple(outs)


def body(train_gate, drift_gate, spread_gate, train_up, drift_up, spread_up, norm_gain):
    hold_gate = hold_rate * drift_gate + spread_gate
    whole_gate = train_gate - learn_rate * hold_gate
    hold_up = hold_rate * drift_up + spread_up
    whole_up = train_up - learn_rate * hold_up
    whole_gained_gate = whole_gate * norm_gain[:, None]
    whole_gained_up = whole_up * norm_gain[:, None]
    factor_gate, factor_up = together(
        (jnp.max(jnp.abs(whole_gained_gate), axis=0), jnp.max(jnp.abs(whole_gained_up), axis=0)),
        "zero",
    )
    narrow_gate, narrow_up = (
        (whole_gained_gate / factor_gate).astype(jnp.bfloat16),
        (whole_gained_up / factor_up).astype(jnp.bfloat16),
    )
    serving_gate, serving_up = sent_together((narrow_gate, narrow_up), "zero", 0, 1)
    return (serving_gate, serving_up, factor_gate, factor_up)


def solution(mesh):
    return jax.shard_map(
        body,
        mesh=mesh,
        in_specs=(
            P("zero", "width"),
            P("zero", "width"),
            P("zero", "width"),
            P("zero", "width"),
            P("zero", "width"),
            P("zero", "width"),
            P("zero"),
        ),
        out_specs=(P(None, "width"), P(None, "width"), P("width"), P("width")),
        check_vma=False,
    )
```

profile of v0, /device:TPU:32, one launch (start us, length us, event | category | flops | bytes accessed | tf_op | source)
XLA Modules:
  0.0 199.9 jit_solution(1440838860592052964)
XLA Ops:
  7.2 0.0 all-gather.2.cloned.1.call-start
  7.2 3.5 %abs_reduce_fusion.1 = (f32[864]{0:T(1024)S(1)}, f32[320,864]{1,0:T(8,128)S(1)}, f32[864]{0:T(1024)S(1)}, f32[320,864]{1,0:T(8,128)S(1)}) fusion(f32[320]{0:T(512)} %param.13, f32[320,864]{1,0:T(8,128)} %param.7, f32[320,864]{1,0:T(8,128)} %param.9, f32[320,864]{1,0:T(8,128)} %param.8, f32[320,864]{1,0:T(8,128)} %param.10, f32[320,864]{1,0:T(8,128)} %param.12, ...), kind=kLoop, calls=%fused_computation.5 | loop fusion | flops 3868992 | bytes 8855552 | tf_op jit(solution)/shard_map/reduce_max | solution.py:46
  10.7 0.1 pad_maximum_fusion.1
  10.8 0.1 broadcast_in_dim.2
  10.9 14.7 %all_to_all.6 = f32[16,1,1728]{2,1,0:T(1,128)S(1)} all-to-all(f32[16,1,1728]{2,1,0:T(1,128)S(1)} %broadcast_in_dim.2), channel_id=1, replica_groups=mesh['zero'=16,'width'=16] {'zero'}, dimensions={0} | all-to-all | bytes 221184 | tf_op jit(solution)/shard_map/all_to_all | solution.py:12
  25.6 0.1 reduce_max.29
  25.7 0.1 fusion.1
  25.7 0.0 copy-start
  25.7 0.0 copy-start.1
  25.7 0.2 divide_convert_fusion
  25.9 0.4 copy-done
  26.3 0.0 copy-done.1
  26.3 1.3 pad_maximum_fusion
  27.6 0.0 all-gather.2.cloned.1.call-update
  27.7 123.3 %all-gather.2.cloned.1.call-done = bf16[5120,1728]{1,0:T(8,128)(2,1)} async-done(((bf16[320,1728]{1,0:T(8,128)(2,1)}), bf16[5120,1728]{1,0:T(8,128)(2,1)}) %all-gather.2.cloned.1.call-update) | async-done | bytes 17694736 | tf_op jit(solution)/shard_map/all_gather | solution.py:31
  150.9 16.7 %fusion = (bf16[5120,864]{1,0:T(8,128)(2,1)}, bf16[5120,864]{1,0:T(8,128)(2,1)}) fusion(bf16[5120,1728]{1,0:T(8,128)(2,1)} %all-gather.2.cloned.1.call-done), kind=kLoop, calls=%fused_computation.8 | loop fusion | bytes 35389440 | tf_op jit(solution)/shard_map/slice | solution.py:33
  167.6 12.7 %copy.23 = bf16[5120,864]{0,1:T(8,128)(2,1)} copy(bf16[5120,864]{1,0:T(8,128)(2,1)} %get-tuple-element.20) | data formatting | bytes 17694720
  180.3 12.7 %copy.22 = bf16[5120,864]{0,1:T(8,128)(2,1)} copy(bf16[5120,864]{1,0:T(8,128)(2,1)} %get-tuple-element.21) | data formatting | bytes 17694720
Async XLA Ops:
  7.2 143.8 %all-gather.2.cloned.1.call-start = ((), (), s32[]{:S(2)}) async-start(), calls=%async_computation.1 | async-start | bytes 19496960 | tf_op jit(solution)/shard_map/all_gather | solution.py:31
  25.7 0.6 copy-start
  25.7 0.6 copy-start.1
Sparse Core Ops, SparseCore 0:
  27.8 123.1 all-gather.1
where the time goes:
time: 202 us; the launch traced here: 200 us
  waiting for transfers between devices  123 us (61%)
  local copies, waits for them, and re-layouts  42.7 us (21%)
  blocking collectives  14.7 us (7%)
  between operations  14.1 us (7%)
  other arithmetic  5.1 us (3%)
    all_gather x1, waiting for transfers between devices, sent_together(): filled, at, outs = (lax.all_gather(both, axis, axis=dim, tiled=True), 0, [])  123 us
    unnamed x6, local copies, waits for them, and re-layouts  25.8 us
    slice x1, local copies, waits for them, and re-layouts, sent_together(): outs.append(lax.slice_in_dim(filled, at, at + a.shape[along], axis=along))  16.7 us
    all_to_all x1, blocking collectives, sent_to_all(): lax.all_to_all(jnp.broadcast_to(array[None], (count, *array.shape)), axis...  14.7 us
  transfers between devices with their start and end apart: 1, of which 1 were waited for; matrix products, arithmetic and copies ran while one was open for 0% of the time, Pallas kernels for 0%

commit v1 on v0

v1 whole, which is shorter than its diff:
```python
import functools

import jax
import jax.numpy as jnp
from jax import lax
from jax.experimental import pallas as pl
from jax.experimental.pallas import tpu as pltpu
from jax.sharding import PartitionSpec as P

learn_rate = 0.3
hold_rate = 0.9

SIDE = 4
GROUP = SIDE * SIDE
ROWS = 320
COLS = 864
LANES = 128
TILES = 7
HALF = 64
PIECES = 4
PIECE = COLS // PIECES
FIRST = 112
SECOND = PIECE - FIRST
PACKED = 2 * PIECE + FIRST
ARRAY_PIECES = GROUP * PIECES

OWN_SLOTS = (("f", 1), ("f", 2), (0, 1), (0, 2))
LATER_SLOTS = (
    ("f", 3), (0, 3), (-1, 1), (1, 1), (2, 1), (-1, 2), (-1, 3), (1, 2), (1, 3), (2, 2), (2, 3),
)
LINKS = (("x", 1), ("x", -1), ("y", 1), ("y", -1))


def sent_in(link, slot):
    axis, sign = link
    block, part = slot
    first = 0 if axis == "x" else 1
    half = first if block == "f" else 1 - first
    lead = 0 if sign == 1 else 1
    piece = 2 * half + (1 - lead if part == 2 else lead)
    along = -sign if part == 3 else 0
    across = 0 if block == "f" else block
    dx, dy = (along, across) if axis == "x" else (across, along)
    return dx % SIDE, dy % SIDE, piece


def received_in(link, slot):
    axis, sign = link
    dx, dy, piece = sent_in(link, slot)
    if axis == "x":
        dx = (dx - sign) % SIDE
    else:
        dy = (dy - sign) % SIDE
    return dx, dy, piece


def kernel(
    train_gate, drift_gate, spread_gate, train_up, drift_up, spread_up, gain,
    out_gate, out_up, factor_gate, factor_up,
    train, drift, spread, whole, turned, gains, gain_columns, factor_columns, land, maxima,
    in_sem, gain_sem, max_send, max_recv, send_sem, recv_sem,
):
    me = lax.axis_index("zero")
    my_x, my_y = lax.rem(me, SIDE), me // SIDE

    def device(dx, dy):
        return lax.rem(my_y + dy, SIDE) * SIDE + lax.rem(my_x + dx, SIDE)

    def peer(step):
        return lax.rem(me + step, GROUP)

    sources = ((train_gate, drift_gate, spread_gate), (train_up, drift_up, spread_up))
    outs = (out_gate, out_up)
    factors = (factor_gate, factor_up)

    gain_copy = pltpu.make_async_copy(gain, gains, gain_sem)
    gain_copy.start()
    loads = []
    for a in range(2):
        for k, (source, target) in enumerate(zip(sources[a], (train, drift, spread))):
            copy = pltpu.make_async_copy(source, target.at[a], in_sem.at[a, k])
            copy.start()
            loads.append(copy)

    barrier = pltpu.get_barrier_semaphore()
    for step in range(1, GROUP):
        pl.semaphore_signal(
            barrier, inc=1, device_id={"zero": peer(step)}, device_id_type=pl.DeviceIdType.MESH
        )

    for a in range(2):
        whole[a, :, (TILES - 1) * LANES :] = jnp.zeros((ROWS, LANES), jnp.float32)

    gain_copy.wait()
    for at in range(0, ROWS, LANES):
        count = min(LANES, ROWS - at)
        row = lax.broadcasted_iota(jnp.int32, (count, count), 0)
        column = lax.broadcasted_iota(jnp.int32, (count, count), 1)
        some = gains[at : at + count].reshape(1, count)
        diagonal = jnp.where(row == column, some, 0.0)
        gain_columns[at : at + count, :] = jnp.broadcast_to(
            jnp.sum(diagonal, axis=1, keepdims=True), (count, LANES)
        )

    def tile(c):
        return slice(c * LANES, min((c + 1) * LANES, COLS))

    def step_and_send(a):
        for k in range(3):
            loads[3 * a + k].wait()

        def stripe(i, tops):
            at = pl.ds(pl.multiple_of(i * 8, 8), 8)
            scale = gain_columns[at, :]
            new = []
            for c in range(TILES):
                hold = hold_rate * drift[a, at, tile(c)] + spread[a, at, tile(c)]
                value = (train[a, at, tile(c)] - learn_rate * hold) * scale[:, : hold.shape[1]]
                whole[a, at, tile(c)] = value
                new.append(jnp.maximum(tops[c], jnp.abs(value)))
            return tuple(new)

        tops = lax.fori_loop(
            0,
            ROWS // 8,
            stripe,
            tuple(jnp.zeros((8, min(LANES, COLS - c * LANES)), jnp.float32) for c in range(TILES)),
            unroll=2,
        )
        maxima[a, 0] = jnp.zeros((8, LANES), jnp.float32)
        for c in range(TILES):
            maxima[a, 0, c : c + 1, : tops[c].shape[1]] = jnp.max(tops[c], axis=0, keepdims=True)
        if a == 0:
            pl.semaphore_wait(barrier, GROUP - 1)
        for step in range(1, GROUP):
            pltpu.make_async_remote_copy(
                src_ref=maxima.at[a, 0],
                dst_ref=maxima.at[a, step],
                send_sem=max_send.at[a],
                recv_sem=max_recv.at[a],
                device_id={"zero": peer(step)},
                device_id_type=pl.DeviceIdType.MESH,
            ).start()

    def piece_at(a, dx, dy, piece):
        return a * ARRAY_PIECES + device(dx, dy) * PIECES + piece

    odd = lax.rem(me, 2)

    def turn(a):
        starts = (odd * HALF, odd * HALF + LANES)
        for c in range(TILES):
            columns = slice(c * LANES, (c + 1) * LANES)
            for k, start in enumerate(starts):
                rows = pl.ds(pl.multiple_of(start, HALF), LANES)
                turned[a, columns, k * LANES : (k + 1) * LANES] = whole[a, rows, columns].T
            rows = pl.ds(pl.multiple_of((1 - odd) * 4 * HALF, HALF), HALF)
            turned[a, columns, 2 * LANES : 2 * LANES + HALF] = whole[a, rows, columns].T

    def round_own(a):
        rest = maxima.at[a, pl.ds(1, GROUP - 1)]
        pltpu.make_async_copy(rest, rest, max_recv.at[a]).wait()
        factor = jnp.max(maxima[a], axis=0)
        factors[a][...] = factor
        upright = factor.T
        for c in range(TILES):
            factor_columns[c * LANES : (c + 1) * LANES, :] = jnp.broadcast_to(
                upright[:, c : c + 1], (LANES, LANES)
            )
        own = a * ARRAY_PIECES + me * PIECES

        def one(piece, carry):
            start = piece * PIECE
            at = pl.ds(pl.multiple_of(start, 8), PIECE)
            divisor = factor_columns[at, :]
            for k in range(2):
                value = turned[a, at, k * LANES : (k + 1) * LANES] / divisor
                land[own + piece, k * PIECE : (k + 1) * PIECE, :] = value.astype(jnp.bfloat16)
            value = turned[a, at, 2 * LANES :] / divisor
            left = lax.broadcasted_iota(jnp.int32, (SECOND, LANES), 1) < HALF
            both = jnp.where(left, value[:SECOND], pltpu.roll(value[FIRST:], HALF, 1))
            land[own + piece, 2 * PIECE : 2 * PIECE + SECOND, :] = both.astype(jnp.bfloat16)
            land[own + piece, 2 * PIECE + SECOND :, :] = value[SECOND:FIRST].astype(jnp.bfloat16)
            return carry

        lax.fori_loop(0, PIECES, one, 0)

    def send(a, link, slot):
        axis, sign = link
        at = piece_at(a, *sent_in(link, slot))
        towards = device(sign % SIDE, 0) if axis == "x" else device(0, sign % SIDE)
        pltpu.make_async_remote_copy(
            src_ref=land.at[at],
            dst_ref=land.at[at],
            send_sem=send_sem.at[LINKS.index(link)],
            recv_sem=recv_sem.at[at],
            device_id={"zero": towards},
            device_id_type=pl.DeviceIdType.MESH,
        ).start()

    arrived = set()

    def await_piece(a, where):
        if (a, where) in arrived or where[:2] == (0, 0):
            return
        arrived.add((a, where))
        at = piece_at(a, *where)
        pltpu.make_async_copy(land.at[at], land.at[at], recv_sem.at[at]).wait()

    def unpack(a, where):
        await_piece(a, where)
        dx, dy, piece = where
        at = piece_at(a, *where)
        source = device(dx, dy)
        right = lax.rem(source, 2)
        base = (source // 2) * 5 * LANES
        full = pl.multiple_of(base + right * 3 * LANES, LANES)
        shared = pl.multiple_of(base + 2 * LANES, LANES)
        start = piece * PIECE
        for k in range(2):
            outs[a][start : start + PIECE, pl.ds(pl.multiple_of(full + k * LANES, LANES), LANES)] = land[
                at, k * PIECE : (k + 1) * PIECE, :
            ]
        for begin, count, place in ((0, FIRST, 0), (FIRST, SECOND, 1)):
            rows = slice(start + begin, start + begin + count)
            value = land[at, 2 * PIECE : 2 * PIECE + count, :].astype(jnp.float32)
            value = pltpu.roll(value, lax.rem(right + place, 2) * HALF, 1)
            lane = lax.broadcasted_iota(jnp.int32, (count, LANES), 1)
            mine = (lane // HALF) == right
            old = outs[a][rows, pl.ds(shared, LANES)].astype(jnp.float32)
            outs[a][rows, pl.ds(shared, LANES)] = jnp.where(mine, value, old).astype(jnp.bfloat16)

    step_and_send(0)
    step_and_send(1)
    for a in range(2):
        turn(a)
        round_own(a)
        for slot in OWN_SLOTS:
            for link in LINKS:
                send(a, link, slot)
    for a in range(2):
        for piece in range(PIECES):
            unpack(a, (0, 0, piece))

    order = [(a, slot) for a in range(2) for slot in OWN_SLOTS]
    done = 0
    for a, slot in ((a, slot) for a in range(2) for slot in LATER_SLOTS):
        for link in LINKS:
            await_piece(a, sent_in(link, slot))
            send(a, link, slot)
        order.append((a, slot))
        while done < len(order) - 3:
            for link in LINKS:
                unpack(order[done][0], received_in(link, order[done][1]))
            done += 1
    for a, slot in order[done:]:
        for link in LINKS:
            unpack(a, received_in(link, slot))

    for a in range(2):
        rest = maxima.at[a, pl.ds(1, GROUP - 1)]
        pltpu.make_async_copy(rest, rest, max_send.at[a]).wait()
    sent = land.at[pl.ds(0, 2 * (len(OWN_SLOTS) + len(LATER_SLOTS)))]
    for k in range(len(LINKS)):
        pltpu.make_async_copy(sent, sent, send_sem.at[k]).wait()


def body(train_gate, drift_gate, spread_gate, train_up, drift_up, spread_up, norm_gain):
    anywhere = pl.BlockSpec(memory_space=pltpu.HBM)
    near = pl.BlockSpec(memory_space=pltpu.VMEM)
    serving_gate, serving_up, factor_gate, factor_up = pl.pallas_call(
        kernel,
        out_shape=(
            pltpu.VMEM((COLS, GROUP * ROWS), jnp.bfloat16),
            pltpu.VMEM((COLS, GROUP * ROWS), jnp.bfloat16),
            pltpu.VMEM((8, LANES), jnp.float32),
            pltpu.VMEM((8, LANES), jnp.float32),
        ),
        in_specs=[anywhere] * 7,
        out_specs=(near,) * 4,
        scratch_shapes=[
            pltpu.VMEM((2, ROWS, COLS), jnp.float32),
            pltpu.VMEM((2, ROWS, COLS), jnp.float32),
            pltpu.VMEM((2, ROWS, COLS), jnp.float32),
            pltpu.VMEM((2, ROWS, TILES * LANES), jnp.float32),
            pltpu.VMEM((2, TILES * LANES, 3 * LANES), jnp.float32),
            pltpu.VMEM((ROWS,), jnp.float32),
            pltpu.VMEM((ROWS, LANES), jnp.float32),
            pltpu.VMEM((TILES * LANES, LANES), jnp.float32),
            pltpu.VMEM((2 * ARRAY_PIECES, PACKED, LANES), jnp.bfloat16),
            pltpu.VMEM((2, GROUP, 8, LANES), jnp.float32),
            pltpu.SemaphoreType.DMA((2, 3)),
            pltpu.SemaphoreType.DMA,
            pltpu.SemaphoreType.DMA((2,)),
            pltpu.SemaphoreType.DMA((2,)),
            pltpu.SemaphoreType.DMA((len(LINKS),)),
            pltpu.SemaphoreType.DMA((2 * ARRAY_PIECES,)),
        ],
        compiler_params=pltpu.CompilerParams(
            collective_id=0, has_side_effects=True, vmem_limit_bytes=45 << 20
        ),
        name="step_and_gather",
    )(train_gate, drift_gate, spread_gate, train_up, drift_up, spread_up, norm_gain)
    return (
        serving_gate.T,
        serving_up.T,
        factor_gate.reshape(-1)[:COLS],
        factor_up.reshape(-1)[:COLS],
    )


def solution(mesh):
    return jax.shard_map(
        body,
        mesh=mesh,
        in_specs=(P("zero", "width"),) * 6 + (P("zero"),),
        out_specs=(P(None, "width"), P(None, "width"), P("width"), P("width")),
        check_vma=False,
    )
```

time: 202 us -> 112 us (0.55); the launches traced: 200 us -> 112 us
  waiting for transfers between devices: 123 us -> 0 us
  Pallas kernels: 0 us -> 103 us
  local copies, waits for them, and re-layouts: 42.7 us -> 8.28 us
  blocking collectives: 14.7 us -> 0 us
  between operations: 14.1 us -> 0.64 us
  other arithmetic: 5.1 us -> 0 us
    all_gather x1 -> x0, waiting for transfers between devices: 123 us -> none  [sent_together(): filled, at, outs = (lax.all_gather(both, axis, axis=dim, tiled=True), 0, [])]
    pallas_call x0 -> x1, Pallas kernels: none -> 103 us  [body(): pl.pallas_call(kernel, out_shape=(pltpu.VMEM((COLS, GROUP * ROWS), jnp.bf...]
    unnamed x6 -> x4, local copies, waits for them, and re-layouts: 25.8 us -> 8.28 us
    slice x2 -> x0, local copies, waits for them, and re-layouts: 16.8 us -> none  [the longest x1 16.7 us: sent_together(): outs.append(lax.slice_in_dim(filled, at, at + a.shape[along], axis=along))]
    all_to_all x1 -> x0, blocking collectives: 14.7 us -> none  [sent_to_all(): lax.all_to_all(jnp.broadcast_to(array[None], (count, *array.shape)), axis...]
    reduce_max x2 -> x0, other arithmetic: 3.57 us -> none  [the longest x1 3.49 us: body(): jnp.max(jnp.abs(whole_gained_gate), axis=0)]
  transfers between devices with their start and end apart: 1 -> 0, of which waited for: 1 -> 0; matrix products, arithmetic and copies ran while one was open for 0% -> 0% of each run, Pallas kernels for 0% -> 0%
where the time goes in v1:
time: 112 us
  Pallas kernels  103 us (92%)
  local copies, waits for them, and re-layouts  8.28 us (7%)
    pallas_call x1, Pallas kernels, body(): pl.pallas_call(kernel, out_shape=(pltpu.VMEM((COLS, GROUP * ROWS), jnp.bf...  103 us
    unnamed x4, local copies, waits for them, and re-layouts  8.28 us

profile of v1, /device:TPU:32, one launch (start us, length us, event | category | flops | bytes accessed | tf_op | source)
XLA Modules:
  0.0 112.3 jit_solution(8598897298421532165)
XLA Ops:
  0.6 103.4 %step_and_gather.1 = (bf16[864,5120]{1,0:T(8,128)(2,1)S(1)}, bf16[864,5120]{1,0:T(8,128)(2,1)S(1)}, f32[8,128]{1,0:T(8,128)S(1)}, f32[8,128]{1,0:T(8,128)S(1)}) custom-call(f32[320,864]{1,0:T(8,128)} %train_gate.1, f32[320,864]{1,0:T(8,128)} %drift_gate.1, f32[320,864]{1,0:T(8,128)} %spread_gate.1, f32[320,864]{1,0:T(8,128)} %train_up.1, ...), custom_call_target="tpu_custom_call" | custom-call | tf_op jit(solution)/shard_map/step_and_gather/pallas_call | solution.py:271
  104.1 3.6 %copy.15 = bf16[5120,864]{0,1:T(8,128)(2,1)} copy(bf16[5120,864]{0,1:T(8,128)(2,1)S(1)} %bitcast.7) | data formatting | bytes 17694720
  107.6 3.5 %copy.16 = bf16[5120,864]{0,1:T(8,128)(2,1)} copy(bf16[5120,864]{0,1:T(8,128)(2,1)S(1)} %bitcast.6) | data formatting | bytes 17694720
  111.2 0.6 copy.17
  111.7 0.6 copy.18

commit v2 on v1

--- a/solution.py
+++ b/solution.py
@@ -18,17 +18,25 @@
 TILES = 7
 HALF = 64
 PIECES = 4
-PIECE = COLS // PIECES
-FIRST = 112
-SECOND = PIECE - FIRST
-PACKED = 2 * PIECE + FIRST
+SIZES = ((224, 208, 208, 224), (208, 224, 224, 208))
+STARTS = tuple(tuple(sum(sizes[:k]) for k in range(PIECES)) for sizes in SIZES)
+LARGEST = max(SIZES[0]) * 5 // 2
 ARRAY_PIECES = GROUP * PIECES
+OUT_PARTS = 4
 
 OWN_SLOTS = (("f", 1), ("f", 2), (0, 1), (0, 2))
 LATER_SLOTS = (
     ("f", 3), (0, 3), (-1, 1), (1, 1), (2, 1), (-1, 2), (-1, 3), (1, 2), (1, 3), (2, 2), (2, 3),
 )
 LINKS = (("x", 1), ("x", -1), ("y", 1), ("y", -1))
+LINK_SLOTS = len(OWN_SLOTS) + len(LATER_SLOTS)
+
+
+def hops(peer):
+    return sum(min(d, SIDE - d) for d in peer)
+
+
+PEERS = sorted(((dx, dy) for dx in range(SIDE) for dy in range(SIDE)), key=hops)[:0:-1]
 
 
 def sent_in(link, slot):
@@ -66,9 +74,6 @@
     def device(dx, dy):
         return lax.rem(my_y + dy, SIDE) * SIDE + lax.rem(my_x + dx, SIDE)
 
-    def peer(step):
-        return lax.rem(me + step, GROUP)
-
     sources = ((train_gate, drift_gate, spread_gate), (train_up, drift_up, spread_up))
     outs = (out_gate, out_up)
     factors = (factor_gate, factor_up)
@@ -78,14 +83,17 @@
     loads = []
     for a in range(2):
         for k, (source, target) in enumerate(zip(sources[a], (train, drift, spread))):
-            copy = pltpu.make_async_copy(source, target.at[a], in_sem.at[a, k])
-            copy.start()
-            loads.append(copy)
+            loads.append(pltpu.make_async_copy(source, target.at[a], in_sem.at[a, k]))
+    for copy in loads[:3]:
+        copy.start()
 
     barrier = pltpu.get_barrier_semaphore()
-    for step in range(1, GROUP):
+    for peer in PEERS:
         pl.semaphore_signal(
-            barrier, inc=1, device_id={"zero": peer(step)}, device_id_type=pl.DeviceIdType.MESH
+            barrier,
+            inc=1,
+            device_id={"zero": device(*peer)},
+            device_id_type=pl.DeviceIdType.MESH,
         )
 
     for a in range(2):
@@ -108,6 +116,9 @@
     def step_and_send(a):
         for k in range(3):
             loads[3 * a + k].wait()
+        if a == 0:
+            for copy in loads[3:]:
+                copy.start()
 
         def stripe(i, tops):
             at = pl.ds(pl.multiple_of(i * 8, 8), 8)
@@ -132,13 +143,13 @@
             maxima[a, 0, c : c + 1, : tops[c].shape[1]] = jnp.max(tops[c], axis=0, keepdims=True)
         if a == 0:
             pl.semaphore_wait(barrier, GROUP - 1)
-        for step in range(1, GROUP):
+        for dx, dy in PEERS:
             pltpu.make_async_remote_copy(
                 src_ref=maxima.at[a, 0],
-                dst_ref=maxima.at[a, step],
+                dst_ref=maxima.at[a, dy * SIDE + dx],
                 send_sem=max_send.at[a],
                 recv_sem=max_recv.at[a],
-                device_id={"zero": peer(step)},
+                device_id={"zero": device(dx, dy)},
                 device_id_type=pl.DeviceIdType.MESH,
             ).start()
 
@@ -157,7 +168,7 @@
             rows = pl.ds(pl.multiple_of((1 - odd) * 4 * HALF, HALF), HALF)
             turned[a, columns, 2 * LANES : 2 * LANES + HALF] = whole[a, rows, columns].T
 
-    def round_own(a):
+    def take_factor(a):
         rest = maxima.at[a, pl.ds(1, GROUP - 1)]
         pltpu.make_async_copy(rest, rest, max_recv.at[a]).wait()
         factor = jnp.max(maxima[a], axis=0)
@@ -167,45 +178,47 @@
             factor_columns[c * LANES : (c + 1) * LANES, :] = jnp.broadcast_to(
                 upright[:, c : c + 1], (LANES, LANES)
             )
-        own = a * ARRAY_PIECES + me * PIECES
-
-        def one(piece, carry):
-            start = piece * PIECE
-            at = pl.ds(pl.multiple_of(start, 8), PIECE)
-            divisor = factor_columns[at, :]
-            for k in range(2):
-                value = turned[a, at, k * LANES : (k + 1) * LANES] / divisor
-                land[own + piece, k * PIECE : (k + 1) * PIECE, :] = value.astype(jnp.bfloat16)
-            value = turned[a, at, 2 * LANES :] / divisor
-            left = lax.broadcasted_iota(jnp.int32, (SECOND, LANES), 1) < HALF
-            both = jnp.where(left, value[:SECOND], pltpu.roll(value[FIRST:], HALF, 1))
-            land[own + piece, 2 * PIECE : 2 * PIECE + SECOND, :] = both.astype(jnp.bfloat16)
-            land[own + piece, 2 * PIECE + SECOND :, :] = value[SECOND:FIRST].astype(jnp.bfloat16)
-            return carry
-
-        lax.fori_loop(0, PIECES, one, 0)
+
+    def round_piece(a, piece):
+        at = piece_at(a, 0, 0, piece)
+        size, start = SIZES[a][piece], STARTS[a][piece]
+        columns = slice(start, start + size)
+        divisor = factor_columns[columns, :]
+        for k in range(2):
+            value = turned[a, columns, k * LANES : (k + 1) * LANES] / divisor
+            land[at, k * size : (k + 1) * size, :] = value.astype(jnp.bfloat16)
+        value = turned[a, columns, 2 * LANES :] / divisor
+        left = lax.broadcasted_iota(jnp.int32, (size // 2, LANES), 1) < HALF
+        both = jnp.where(left, value[: size // 2], pltpu.roll(value[size // 2 :], HALF, 1))
+        land[at, 2 * size : size * 5 // 2, :] = both.astype(jnp.bfloat16)
 
     def send(a, link, slot):
         axis, sign = link
-        at = piece_at(a, *sent_in(link, slot))
+        where = sent_in(link, slot)
         towards = device(sign % SIDE, 0) if axis == "x" else device(0, sign % SIDE)
-        pltpu.make_async_remote_copy(
-            src_ref=land.at[at],
-            dst_ref=land.at[at],
-            send_sem=send_sem.at[LINKS.index(link)],
-            recv_sem=recv_sem.at[at],
+        copy = pltpu.make_async_remote_copy(
+            src_ref=held(a, where),
+            dst_ref=held(a, where),
+            send_sem=send_sem.at[len(sends)],
+            recv_sem=recv_sem.at[piece_at(a, *where)],
             device_id={"zero": towards},
             device_id_type=pl.DeviceIdType.MESH,
-        ).start()
-
+        )
+        copy.start()
+        sends.append(copy)
+
+    def held(a, where):
+        return land.at[piece_at(a, *where), pl.ds(0, SIZES[a][where[2]] * 5 // 2)]
+
+    sends = []
     arrived = set()
 
     def await_piece(a, where):
         if (a, where) in arrived or where[:2] == (0, 0):
             return
         arrived.add((a, where))
-        at = piece_at(a, *where)
-        pltpu.make_async_copy(land.at[at], land.at[at], recv_sem.at[at]).wait()
+        ref = held(a, where)
+        pltpu.make_async_copy(ref, ref, recv_sem.at[piece_at(a, *where)]).wait()
 
     def unpack(a, where):
         await_piece(a, where)
@@ -216,14 +229,15 @@
         base = (source // 2) * 5 * LANES
         full = pl.multiple_of(base + right * 3 * LANES, LANES)
         shared = pl.multiple_of(base + 2 * LANES, LANES)
-        start = piece * PIECE
+        size, start = SIZES[a][piece], STARTS[a][piece]
+        count = size // 2
         for k in range(2):
-            outs[a][start : start + PIECE, pl.ds(pl.multiple_of(full + k * LANES, LANES), LANES)] = land[
-                at, k * PIECE : (k + 1) * PIECE, :
+            outs[a][start : start + size, pl.ds(pl.multiple_of(full + k * LANES, LANES), LANES)] = land[
+                at, k * size : (k + 1) * size, :
             ]
-        for begin, count, place in ((0, FIRST, 0), (FIRST, SECOND, 1)):
-            rows = slice(start + begin, start + begin + count)
-            value = land[at, 2 * PIECE : 2 * PIECE + count, :].astype(jnp.float32)
+        for place in range(2):
+            rows = slice(start + place * count, start + (place + 1) * count)
+            value = land[at, 2 * size : 2 * size + count, :].astype(jnp.float32)
             value = pltpu.roll(value, lax.rem(right + place, 2) * HALF, 1)
             lane = lax.broadcasted_iota(jnp.int32, (count, LANES), 1)
             mine = (lane // HALF) == right
@@ -234,8 +248,13 @@
     step_and_send(1)
     for a in range(2):
         turn(a)
-        round_own(a)
-        for slot in OWN_SLOTS:
+        take_factor(a)
+        for piece in (0, 2, 1, 3):
+            round_piece(a, piece)
+            for link in LINKS:
+                if sent_in(link, OWN_SLOTS[0])[2] == piece:
+                    send(a, link, OWN_SLOTS[0])
+        for slot in OWN_SLOTS[1:]:
             for link in LINKS:
                 send(a, link, slot)
     for a in range(2):
@@ -260,15 +279,30 @@
     for a in range(2):
         rest = maxima.at[a, pl.ds(1, GROUP - 1)]
         pltpu.make_async_copy(rest, rest, max_send.at[a]).wait()
-    sent = land.at[pl.ds(0, 2 * (len(OWN_SLOTS) + len(LATER_SLOTS)))]
-    for k in range(len(LINKS)):
-        pltpu.make_async_copy(sent, sent, send_sem.at[k]).wait()
+    for copy in sends:
+        copy.wait_send()
+
+
+def copy_out(gate, up, factor_gate, factor_up, to_gate, to_up, to_factor_gate, to_factor_up, sems):
+    copies = []
+    for source, target in ((factor_gate, to_factor_gate), (factor_up, to_factor_up)):
+        copies.append(pltpu.make_async_copy(source, target, sems.at[len(copies)]))
+    for part in range(OUT_PARTS):
+        rows = pl.ds(part * (COLS // OUT_PARTS), COLS // OUT_PARTS)
+        for source, target in ((gate, to_gate), (up, to_up)):
+            copies.append(
+                pltpu.make_async_copy(source.at[rows], target.at[rows], sems.at[len(copies)])
+            )
+    for copy in copies:
+        copy.start()
+    for copy in copies:
+        copy.wait()
 
 
 def body(train_gate, drift_gate, spread_gate, train_up, drift_up, spread_up, norm_gain):
     anywhere = pl.BlockSpec(memory_space=pltpu.HBM)
     near = pl.BlockSpec(memory_space=pltpu.VMEM)
-    serving_gate, serving_up, factor_gate, factor_up = pl.pallas_call(
+    results = pl.pallas_call(
         kernel,
         out_shape=(
             pltpu.VMEM((COLS, GROUP * ROWS), jnp.bfloat16),
@@ -287,13 +321,13 @@
             pltpu.VMEM((ROWS,), jnp.float32),
             pltpu.VMEM((ROWS, LANES), jnp.float32),
             pltpu.VMEM((TILES * LANES, LANES), jnp.float32),
-            pltpu.VMEM((2 * ARRAY_PIECES, PACKED, LANES), jnp.bfloat16),
+            pltpu.VMEM((2 * ARRAY_PIECES, LARGEST, LANES), jnp.bfloat16),
             pltpu.VMEM((2, GROUP, 8, LANES), jnp.float32),
             pltpu.SemaphoreType.DMA((2, 3)),
             pltpu.SemaphoreType.DMA,
             pltpu.SemaphoreType.DMA((2,)),
             pltpu.SemaphoreType.DMA((2,)),
-            pltpu.SemaphoreType.DMA((len(LINKS),)),
+            pltpu.SemaphoreType.DMA((2 * len(LINKS) * LINK_SLOTS,)),
             pltpu.SemaphoreType.DMA((2 * ARRAY_PIECES,)),
         ],
         compiler_params=pltpu.CompilerParams(
@@ -301,6 +335,21 @@
         ),
         name="step_and_gather",
     )(train_gate, drift_gate, spread_gate, train_up, drift_up, spread_up, norm_gain)
+    far = pl.BlockSpec(memory_space=pltpu.HBM)
+    serving_gate, serving_up, factor_gate, factor_up = pl.pallas_call(
+        copy_out,
+        out_shape=(
+            jax.ShapeDtypeStruct((COLS, GROUP * ROWS), jnp.bfloat16),
+            jax.ShapeDtypeStruct((COLS, GROUP * ROWS), jnp.bfloat16),
+            jax.ShapeDtypeStruct((8, LANES), jnp.float32),
+            jax.ShapeDtypeStruct((8, LANES), jnp.float32),
+        ),
+        in_specs=[pl.BlockSpec(memory_space=pl.ANY)] * 4,
+        out_specs=(far,) * 4,
+        scratch_shapes=[pltpu.SemaphoreType.DMA((2 + 2 * OUT_PARTS,))],
+        compiler_params=pltpu.CompilerParams(vmem_limit_bytes=1 << 20),
+        name="copy_out",
+    )(*results)
     return (
         serving_gate.T,
         serving_up.T,

time: 112 us -> 110 us (0.982)
  local copies, waits for them, and re-layouts: 8.28 us -> 0 us
  Pallas kernels: 103 us -> 109 us
    unnamed x4 -> x0, local copies, waits for them, and re-layouts: 8.28 us -> none
    pallas_call x0 -> x1, Pallas kernels: none -> 6.23 us  [body(): pl.pallas_call(copy_out, out_shape=(jax.ShapeDtypeStruct((COLS, GROUP * R...]
where the time goes in v2:
time: 110 us
  Pallas kernels  109 us (99%)
    pallas_call x1, Pallas kernels, body(): pl.pallas_call(kernel, out_shape=(pltpu.VMEM((COLS, GROUP * ROWS), jnp.bf...  103 us
    pallas_call x1, Pallas kernels, body(): pl.pallas_call(copy_out, out_shape=(jax.ShapeDtypeStruct((COLS, GROUP * R...  6.23 us

profile of v2, /device:TPU:32, one launch (start us, length us, event | category | flops | bytes accessed | tf_op | source)
XLA Modules:
  0.0 110.1 jit_solution(14281062856680966405)
XLA Ops:
  0.6 103.2 %step_and_gather.1 = (bf16[864,5120]{1,0:T(8,128)(2,1)S(1)}, bf16[864,5120]{1,0:T(8,128)(2,1)S(1)}, f32[8,128]{1,0:T(8,128)S(1)}, f32[8,128]{1,0:T(8,128)S(1)}) custom-call(f32[320,864]{1,0:T(8,128)} %train_gate.1, f32[320,864]{1,0:T(8,128)} %drift_gate.1, f32[320,864]{1,0:T(8,128)} %spread_gate.1, f32[320,864]{1,0:T(8,128)} %train_up.1, ...), custom_call_target="tpu_custom_call" | custom-call | tf_op jit(solution)/shard_map/step_and_gather/pallas_call | solution.py:305
  103.9 6.2 %copy_out.1 = (bf16[864,5120]{1,0:T(8,128)(2,1)}, bf16[864,5120]{1,0:T(8,128)(2,1)}, f32[8,128]{1,0:T(8,128)}, f32[8,128]{1,0:T(8,128)}) custom-call(bf16[864,5120]{1,0:T(8,128)(2,1)S(1)} %get-tuple-element.12.gate, bf16[864,5120]{1,0:T(8,128)(2,1)S(1)} %get-tuple-element.13.up, f32[8,128]{1,0:T(8,128)S(1)} %get-tuple-element.14.factor_gate, ...), custom_call_target="tpu_custom_call" | custom-call | tf_op jit(solution)/shard_map/copy_out/pallas_call | solution.py:339

commit v3 on v2

--- a/solution.py
+++ b/solution.py
@@ -23,6 +23,7 @@
 LARGEST = max(SIZES[0]) * 5 // 2
 ARRAY_PIECES = GROUP * PIECES
 OUT_PARTS = 4
+EARLY = 1
 
 OWN_SLOTS = (("f", 1), ("f", 2), (0, 1), (0, 2))
 LATER_SLOTS = (
@@ -65,8 +66,8 @@
 def kernel(
     train_gate, drift_gate, spread_gate, train_up, drift_up, spread_up, gain,
     out_gate, out_up, factor_gate, factor_up,
-    train, drift, spread, whole, turned, gains, gain_columns, factor_columns, land, maxima,
-    in_sem, gain_sem, max_send, max_recv, send_sem, recv_sem,
+    train, drift, spread, whole, turned, early, gains, gain_columns, factor_columns, land, maxima,
+    in_sem, gain_sem, max_send, max_recv, send_sem, recv_sem, early_sem,
 ):
     me = lax.axis_index("zero")
     my_x, my_y = lax.rem(me, SIDE), me // SIDE
@@ -95,9 +96,6 @@
             device_id={"zero": device(*peer)},
             device_id_type=pl.DeviceIdType.MESH,
         )
-
-    for a in range(2):
-        whole[a, :, (TILES - 1) * LANES :] = jnp.zeros((ROWS, LANES), jnp.float32)
 
     gain_copy.wait()
     for at in range(0, ROWS, LANES):
@@ -113,7 +111,7 @@
     def tile(c):
         return slice(c * LANES, min((c + 1) * LANES, COLS))
 
-    def step_and_send(a):
+    def step(a):
         for k in range(3):
             loads[3 * a + k].wait()
         if a == 0:
@@ -141,8 +139,8 @@
         maxima[a, 0] = jnp.zeros((8, LANES), jnp.float32)
         for c in range(TILES):
             maxima[a, 0, c : c + 1, : tops[c].shape[1]] = jnp.max(tops[c], axis=0, keepdims=True)
-        if a == 0:
-            pl.semaphore_wait(barrier, GROUP - 1)
+
+    def send_maxima(a):
         for dx, dy in PEERS:
             pltpu.make_async_remote_copy(
                 src_ref=maxima.at[a, 0],
@@ -158,15 +156,32 @@
 
     odd = lax.rem(me, 2)
 
-    def turn(a):
+    def turn(a, tiles):
         starts = (odd * HALF, odd * HALF + LANES)
-        for c in range(TILES):
+        for c in tiles:
             columns = slice(c * LANES, (c + 1) * LANES)
-            for k, start in enumerate(starts):
-                rows = pl.ds(pl.multiple_of(start, HALF), LANES)
-                turned[a, columns, k * LANES : (k + 1) * LANES] = whole[a, rows, columns].T
+            values = []
+            for begin in starts:
+                rows = pl.ds(pl.multiple_of(begin, HALF), LANES)
+                values.append(whole[a, rows, columns].T)
             rows = pl.ds(pl.multiple_of((1 - odd) * 4 * HALF, HALF), HALF)
-            turned[a, columns, 2 * LANES : 2 * LANES + HALF] = whole[a, rows, columns].T
+            half = whole[a, rows, columns]
+            values.append(jnp.concatenate([half, half], axis=0).T)
+            for piece in range(PIECES):
+                size, start = SIZES[a][piece], STARTS[a][piece]
+                for place in range(2):
+                    first = start + place * (size // 2)
+                    low = max(first, c * LANES)
+                    high = min(first + size // 2, (c + 1) * LANES)
+                    if low >= high:
+                        continue
+                    taken = slice(low - c * LANES, high - c * LANES)
+                    for k in range(2):
+                        at = k * size + low - start
+                        turned[a, piece, at : at + high - low, :] = values[k][taken]
+                    at = 2 * size + low - first
+                    lanes = slice(place * HALF, (place + 1) * HALF)
+                    turned[a, piece, at : at + high - low, lanes] = values[2][taken, lanes]
 
     def take_factor(a):
         rest = maxima.at[a, pl.ds(1, GROUP - 1)]
@@ -175,38 +190,62 @@
         factors[a][...] = factor
         upright = factor.T
         for c in range(TILES):
-            factor_columns[c * LANES : (c + 1) * LANES, :] = jnp.broadcast_to(
+            factor_columns[a, c * LANES : (c + 1) * LANES, :] = jnp.broadcast_to(
                 upright[:, c : c + 1], (LANES, LANES)
             )
 
-    def round_piece(a, piece):
-        at = piece_at(a, 0, 0, piece)
+    def round_blocks(a, source, where, blocks):
+        at, piece = piece_at(a, *where), where[2]
         size, start = SIZES[a][piece], STARTS[a][piece]
-        columns = slice(start, start + size)
-        divisor = factor_columns[columns, :]
-        for k in range(2):
-            value = turned[a, columns, k * LANES : (k + 1) * LANES] / divisor
+        divisor = factor_columns[a, start : start + size, :]
+        for k in blocks:
+            value = source[k * size : (k + 1) * size, :] / divisor
             land[at, k * size : (k + 1) * size, :] = value.astype(jnp.bfloat16)
-        value = turned[a, columns, 2 * LANES :] / divisor
+
+    def round_piece(a, source, where):
+        round_blocks(a, source, where, range(2))
+        at, piece = piece_at(a, *where), where[2]
+        size, start = SIZES[a][piece], STARTS[a][piece]
+        divisor = factor_columns[a, start : start + size, :]
         left = lax.broadcasted_iota(jnp.int32, (size // 2, LANES), 1) < HALF
-        both = jnp.where(left, value[: size // 2], pltpu.roll(value[size // 2 :], HALF, 1))
-        land[at, 2 * size : size * 5 // 2, :] = both.astype(jnp.bfloat16)
-
-    def send(a, link, slot):
+        value = source[2 * size : size * 5 // 2, :]
+        value = value / jnp.where(left, divisor[: size // 2], divisor[size // 2 :])
+        land[at, 2 * size : size * 5 // 2, :] = value.astype(jnp.bfloat16)
+
+    def start_send(link, source, target, arrival):
         axis, sign = link
-        where = sent_in(link, slot)
         towards = device(sign % SIDE, 0) if axis == "x" else device(0, sign % SIDE)
         copy = pltpu.make_async_remote_copy(
-            src_ref=held(a, where),
-            dst_ref=held(a, where),
+            src_ref=source,
+            dst_ref=target,
             send_sem=send_sem.at[len(sends)],
-            recv_sem=recv_sem.at[piece_at(a, *where)],
+            recv_sem=arrival,
             device_id={"zero": towards},
             device_id_type=pl.DeviceIdType.MESH,
         )
         copy.start()
         sends.append(copy)
 
+    def send(a, link, slot):
+        where = sent_in(link, slot)
+        start_send(link, held(a, where), held(a, where), recv_sem.at[piece_at(a, *where)])
+
+    def early_ref(link, piece):
+        return early.at[LINKS.index(link), pl.ds(0, EARLY * SIZES[0][piece])]
+
+    def rest_of(where):
+        size = SIZES[0][where[2]]
+        return land.at[piece_at(0, *where), pl.ds(EARLY * size, size * 5 // 2 - EARLY * size)]
+
+    def send_rest(link):
+        where = sent_in(link, OWN_SLOTS[0])
+        start_send(link, rest_of(where), rest_of(where), recv_sem.at[piece_at(0, *where)])
+
+    def send_early(link):
+        piece = sent_in(link, OWN_SLOTS[0])[2]
+        source = turned.at[0, piece, pl.ds(0, EARLY * SIZES[0][piece])]
+        start_send(link, source, early_ref(link, piece), early_sem.at[LINKS.index(link)])
+
     def held(a, where):
         return land.at[piece_at(a, *where), pl.ds(0, SIZES[a][where[2]] * 5 // 2)]
 
@@ -217,6 +256,14 @@
         if (a, where) in arrived or where[:2] == (0, 0):
             return
         arrived.add((a, where))
+        for k, link in enumerate(LINKS):
+            if (a, where) == (0, received_in(link, OWN_SLOTS[0])):
+                ref = early_ref(link, where[2])
+                pltpu.make_async_copy(ref, ref, early_sem.at[k]).wait()
+                round_blocks(a, early.at[k], where, range(EARLY))
+                ref = rest_of(where)
+                pltpu.make_async_copy(ref, ref, recv_sem.at[piece_at(a, *where)]).wait()
+                return
         ref = held(a, where)
         pltpu.make_async_copy(ref, ref, recv_sem.at[piece_at(a, *where)]).wait()
 
@@ -244,17 +291,26 @@
             old = outs[a][rows, pl.ds(shared, LANES)].astype(jnp.float32)
             outs[a][rows, pl.ds(shared, LANES)] = jnp.where(mine, value, old).astype(jnp.bfloat16)
 
-    step_and_send(0)
-    step_and_send(1)
+    step(0)
+    turn(0, range(4))
+    pl.semaphore_wait(barrier, GROUP - 1)
+    send_maxima(0)
+    for link in LINKS[:2]:
+        send_early(link)
+    turn(0, range(4, TILES))
+    for link in LINKS[2:]:
+        send_early(link)
+    step(1)
+    send_maxima(1)
+    turn(1, range(TILES))
     for a in range(2):
-        turn(a)
         take_factor(a)
-        for piece in (0, 2, 1, 3):
-            round_piece(a, piece)
+        for piece in range(PIECES):
+            round_piece(a, turned.at[a, piece], (0, 0, piece))
+        if a == 0:
             for link in LINKS:
-                if sent_in(link, OWN_SLOTS[0])[2] == piece:
-                    send(a, link, OWN_SLOTS[0])
-        for slot in OWN_SLOTS[1:]:
+                send_rest(link)
+        for slot in OWN_SLOTS[1 - a :]:
             for link in LINKS:
                 send(a, link, slot)
     for a in range(2):
@@ -317,18 +373,20 @@
             pltpu.VMEM((2, ROWS, COLS), jnp.float32),
             pltpu.VMEM((2, ROWS, COLS), jnp.float32),
             pltpu.VMEM((2, ROWS, TILES * LANES), jnp.float32),
-            pltpu.VMEM((2, TILES * LANES, 3 * LANES), jnp.float32),
+            pltpu.VMEM((2, PIECES, LARGEST, LANES), jnp.float32),
+            pltpu.VMEM((len(LINKS), EARLY * max(SIZES[0]), LANES), jnp.float32),
             pltpu.VMEM((ROWS,), jnp.float32),
             pltpu.VMEM((ROWS, LANES), jnp.float32),
-            pltpu.VMEM((TILES * LANES, LANES), jnp.float32),
+            pltpu.VMEM((2, TILES * LANES, LANES), jnp.float32),
             pltpu.VMEM((2 * ARRAY_PIECES, LARGEST, LANES), jnp.bfloat16),
             pltpu.VMEM((2, GROUP, 8, LANES), jnp.float32),
             pltpu.SemaphoreType.DMA((2, 3)),
             pltpu.SemaphoreType.DMA,
             pltpu.SemaphoreType.DMA((2,)),
             pltpu.SemaphoreType.DMA((2,)),
-            pltpu.SemaphoreType.DMA((2 * len(LINKS) * LINK_SLOTS,)),
+            pltpu.SemaphoreType.DMA(((2 * LINK_SLOTS + 1) * len(LINKS),)),
             pltpu.SemaphoreType.DMA((2 * ARRAY_PIECES,)),
+            pltpu.SemaphoreType.DMA((len(LINKS),)),
         ],
         compiler_params=pltpu.CompilerParams(
             collective_id=0, has_side_effects=True, vmem_limit_bytes=45 << 20

time: 110 us -> 109 us (level)
  no operation moved by 1% of the time
where the time goes in v3:
time: 109 us
  Pallas kernels  108 us (99%)
    pallas_call x1, Pallas kernels, body(): pl.pallas_call(kernel, out_shape=(pltpu.VMEM((COLS, GROUP * ROWS), jnp.bf...  102 us
    pallas_call x1, Pallas kernels, body(): pl.pallas_call(copy_out, out_shape=(jax.ShapeDtypeStruct((COLS, GROUP * R...  6.23 us

profile of v3, /device:TPU:32, one launch (start us, length us, event | category | flops | bytes accessed | tf_op | source)
XLA Modules:
  0.0 109.1 jit_solution(14266409578017250644)
XLA Ops:
  0.6 102.2 %step_and_gather.1 = (bf16[864,5120]{1,0:T(8,128)(2,1)S(1)}, bf16[864,5120]{1,0:T(8,128)(2,1)S(1)}, f32[8,128]{1,0:T(8,128)S(1)}, f32[8,128]{1,0:T(8,128)S(1)}) custom-call(f32[320,864]{1,0:T(8,128)} %train_gate.1, f32[320,864]{1,0:T(8,128)} %drift_gate.1, f32[320,864]{1,0:T(8,128)} %spread_gate.1, f32[320,864]{1,0:T(8,128)} %train_up.1, ...), custom_call_target="tpu_custom_call" | custom-call | tf_op jit(solution)/shard_map/step_and_gather/pallas_call | solution.py:361
  102.9 6.2 %copy_out.1 = (bf16[864,5120]{1,0:T(8,128)(2,1)}, bf16[864,5120]{1,0:T(8,128)(2,1)}, f32[8,128]{1,0:T(8,128)}, f32[8,128]{1,0:T(8,128)}) custom-call(bf16[864,5120]{1,0:T(8,128)(2,1)S(1)} %get-tuple-element.12.gate, bf16[864,5120]{1,0:T(8,128)(2,1)S(1)} %get-tuple-element.13.up, f32[8,128]{1,0:T(8,128)S(1)} %get-tuple-element.14.factor_gate, ...), custom_call_target="tpu_custom_call" | custom-call | tf_op jit(solution)/shard_map/copy_out/pallas_call | solution.py:397

commit v4 on v3

--- a/solution.py
+++ b/solution.py
@@ -202,8 +202,7 @@
             value = source[k * size : (k + 1) * size, :] / divisor
             land[at, k * size : (k + 1) * size, :] = value.astype(jnp.bfloat16)
 
-    def round_piece(a, source, where):
-        round_blocks(a, source, where, range(2))
+    def round_shared(a, source, where):
         at, piece = piece_at(a, *where), where[2]
         size, start = SIZES[a][piece], STARTS[a][piece]
         divisor = factor_columns[a, start : start + size, :]
@@ -305,11 +304,15 @@
     turn(1, range(TILES))
     for a in range(2):
         take_factor(a)
+        late = EARLY if a == 0 else 0
+        for link in LINKS:
+            piece = sent_in(link, OWN_SLOTS[0])[2]
+            round_blocks(a, turned.at[a, piece], (0, 0, piece), range(late, 2))
+            round_shared(a, turned.at[a, piece], (0, 0, piece))
+            if a == 0:
+                send_rest(link)
         for piece in range(PIECES):
-            round_piece(a, turned.at[a, piece], (0, 0, piece))
-        if a == 0:
-            for link in LINKS:
-                send_rest(link)
+            round_blocks(a, turned.at[a, piece], (0, 0, piece), range(late))
         for slot in OWN_SLOTS[1 - a :]:
             for link in LINKS:
                 send(a, link, slot)
@@ -318,7 +321,7 @@
             unpack(a, (0, 0, piece))
 
     order = [(a, slot) for a in range(2) for slot in OWN_SLOTS]
-    done = 0
+    done = waited = 0
     for a, slot in ((a, slot) for a in range(2) for slot in LATER_SLOTS):
         for link in LINKS:
             await_piece(a, sent_in(link, slot))
@@ -328,6 +331,9 @@
             for link in LINKS:
                 unpack(order[done][0], received_in(link, order[done][1]))
             done += 1
+        while waited < len(sends) - 5 * len(LINKS):
+            sends[waited].wait_send()
+            waited += 1
     for a, slot in order[done:]:
         for link in LINKS:
             unpack(a, received_in(link, slot))
@@ -335,7 +341,7 @@
     for a in range(2):
         rest = maxima.at[a, pl.ds(1, GROUP - 1)]
         pltpu.make_async_copy(rest, rest, max_send.at[a]).wait()
-    for copy in sends:
+    for copy in sends[waited:]:
         copy.wait_send()
 
 

time: 109 us -> 109 us (level)
  no operation moved by 1% of the time
where the time goes in v4:
time: 109 us
  Pallas kernels  108 us (99%)
    pallas_call x1, Pallas kernels, body(): pl.pallas_call(kernel, out_shape=(pltpu.VMEM((COLS, GROUP * ROWS), jnp.bf...  102 us
    pallas_call x1, Pallas kernels, body(): pl.pallas_call(copy_out, out_shape=(jax.ShapeDtypeStruct((COLS, GROUP * R...  6.23 us

profile of v4, /device:TPU:32, one launch (start us, length us, event | category | flops | bytes accessed | tf_op | source)
XLA Modules:
  0.0 108.9 jit_solution(13889865212950786148)
XLA Ops:
  0.6 102.1 %step_and_gather.1 = (bf16[864,5120]{1,0:T(8,128)(2,1)S(1)}, bf16[864,5120]{1,0:T(8,128)(2,1)S(1)}, f32[8,128]{1,0:T(8,128)S(1)}, f32[8,128]{1,0:T(8,128)S(1)}) custom-call(f32[320,864]{1,0:T(8,128)} %train_gate.1, f32[320,864]{1,0:T(8,128)} %drift_gate.1, f32[320,864]{1,0:T(8,128)} %spread_gate.1, f32[320,864]{1,0:T(8,128)} %train_up.1, ...), custom_call_target="tpu_custom_call" | custom-call | tf_op jit(solution)/shard_map/step_and_gather/pallas_call | solution.py:367
  102.7 6.2 %copy_out.1 = (bf16[864,5120]{1,0:T(8,128)(2,1)}, bf16[864,5120]{1,0:T(8,128)(2,1)}, f32[8,128]{1,0:T(8,128)}, f32[8,128]{1,0:T(8,128)}) custom-call(bf16[864,5120]{1,0:T(8,128)(2,1)S(1)} %get-tuple-element.12.gate, bf16[864,5120]{1,0:T(8,128)(2,1)S(1)} %get-tuple-element.13.up, f32[8,128]{1,0:T(8,128)S(1)} %get-tuple-element.14.factor_gate, ...), custom_call_target="tpu_custom_call" | custom-call | tf_op jit(solution)/shard_map/copy_out/pallas_call | solution.py:403

commit v5 on v4

--- a/solution.py
+++ b/solution.py
@@ -134,7 +134,7 @@
             ROWS // 8,
             stripe,
             tuple(jnp.zeros((8, min(LANES, COLS - c * LANES)), jnp.float32) for c in range(TILES)),
-            unroll=2,
+            unroll=4,
         )
         maxima[a, 0] = jnp.zeros((8, LANES), jnp.float32)
         for c in range(TILES):

time: 109 us -> 109 us (level)
  no operation moved by 1% of the time
where the time goes in v5:
time: 109 us
  Pallas kernels  108 us (99%)
    pallas_call x1, Pallas kernels, body(): pl.pallas_call(kernel, out_shape=(pltpu.VMEM((COLS, GROUP * ROWS), jnp.bf...  102 us
    pallas_call x1, Pallas kernels, body(): pl.pallas_call(copy_out, out_shape=(jax.ShapeDtypeStruct((COLS, GROUP * R...  6.23 us

profile of v5, /device:TPU:32, one launch (start us, length us, event | category | flops | bytes accessed | tf_op | source)
XLA Modules:
  0.0 108.9 jit_solution(7621154640855441222)
XLA Ops:
  0.6 102.0 %step_and_gather.1 = (bf16[864,5120]{1,0:T(8,128)(2,1)S(1)}, bf16[864,5120]{1,0:T(8,128)(2,1)S(1)}, f32[8,128]{1,0:T(8,128)S(1)}, f32[8,128]{1,0:T(8,128)S(1)}) custom-call(f32[320,864]{1,0:T(8,128)} %train_gate.1, f32[320,864]{1,0:T(8,128)} %drift_gate.1, f32[320,864]{1,0:T(8,128)} %spread_gate.1, f32[320,864]{1,0:T(8,128)} %train_up.1, ...), custom_call_target="tpu_custom_call" | custom-call | tf_op jit(solution)/shard_map/step_and_gather/pallas_call | solution.py:367
  102.7 6.2 %copy_out.1 = (bf16[864,5120]{1,0:T(8,128)(2,1)}, bf16[864,5120]{1,0:T(8,128)(2,1)}, f32[8,128]{1,0:T(8,128)}, f32[8,128]{1,0:T(8,128)}) custom-call(bf16[864,5120]{1,0:T(8,128)(2,1)S(1)} %get-tuple-element.12.gate, bf16[864,5120]{1,0:T(8,128)(2,1)S(1)} %get-tuple-element.13.up, f32[8,128]{1,0:T(8,128)S(1)} %get-tuple-element.14.factor_gate, ...), custom_call_target="tpu_custom_call" | custom-call | tf_op jit(solution)/shard_map/copy_out/pallas_call | solution.py:403
